TPU v7x, 32 devices: a whole 2x2x4 slice. The times are simulated.
32 devices in a mesh: wide: 8 (over y, x, core), narrow: 4 (over z).
Axes of the slice: x: 2, y: 2, z: 4, core: 2. Of those that a mesh axis runs over, the one named last changes fastest.
Arguments:
- feat_queries: bfloat16 [8192, 256], P(('wide', 'narrow')), may hold values from -6 to 6
- feat_keys: bfloat16 [8192, 256], P(('wide', 'narrow')), may hold values from -6 to 6
- values: bfloat16 [8192, 1024], P(('wide', 'narrow')), may hold values from -8 to 8
- window_queries: bfloat16 [8192, 1024], P(('wide', 'narrow')), may hold values from -150 to 150
- window_keys: bfloat16 [8192, 1024], P(('wide', 'narrow')), may hold values from -5 to 5
Outputs:
- mixed: bfloat16 [8192, 1024], P(('wide', 'narrow'))
All inputs are finite; a program needn't handle non-finite values.
Results may differ from a plain program's by a relative error of at most 0.0004.
The roundings to bfloat16 on the way count: a program that leaves them out, or rounds other values in their place, can miss the bound.
Values may be sent and summed in bfloat16 or wider, within the bound.
A program may use at most 64 MiB of HBM per device.

v0:
```python
import functools

import jax
import jax.numpy as jnp
import numpy as np
from jax import lax
from jax.experimental import pallas as pl
from jax.experimental.pallas import tpu as pltpu
from jax.sharding import PartitionSpec as P

HEADS = 16
WINDOW = 256
LANES = 128
EARLY = 8
LAG = 2
MESH = pl.DeviceIdType.MESH
F32 = jnp.float32
BF16 = jnp.bfloat16
NT = (((1,), (1,)), ((), ()))


def nt(a, b):
    return lax.dot_general(a, b, NT, preferred_element_type=F32)


def nn(a, b):
    return jnp.dot(a, b, preferred_element_type=F32)


def tables(width):
    first, second = np.triu_indices(width)
    feats = 1 + width + len(first)
    padded = -(-(feats + 4) // 8) * 8
    per = LANES // width
    one = np.zeros((padded, width))
    two = np.zeros((padded, width))
    extra = np.zeros((8, padded))
    extra[0, 0] = 1.0
    extra[1, : 1 + width] = 1.0
    extra[2, 0] = 1.0
    extra[2, 1 : 1 + width] = 1.0 / width**0.25
    for i in range(width):
        one[1 + i, i] = 1.0
    at = 1 + width
    for n, (i, j) in enumerate(zip(first, second)):
        one[at + n, i] = 1.0
        two[at + n, j] = 1.0
        extra[2, at + n] = 1.0 / np.sqrt(2.0 * width) if i == j else 1.0 / np.sqrt(1.0 * width)
    pick = np.zeros((2, per, padded, LANES))
    for j in range(per):
        pick[0, j, :, j * width : (j + 1) * width] = one
        pick[1, j, :, j * width : (j + 1) * width] = two
    return feats, padded, per, pick, extra


def kernel(
    dims,
    fq_in, fk_in, val_in, wq_in, wk_in, pick_in, crow_in, ccol_in,
    out,
    fq, fk, val, wq, wk, pick, crow, ccol,
    qf, kft, state, got, upin, upout, downin, downout, scan, prior, rimk, rimv, num, den, held,
    load, send1, recv1, send2, recv2, usend, urecv, dsend, drecv, rsend, rrecv,
):
    wide, narrow, feats, padded, per, share = dims
    n = wide * narrow
    rows = val.shape[0]
    pairs = val.shape[1] // LANES
    mw = lax.axis_index("wide")
    mz = lax.axis_index("narrow")
    me = mw * narrow + mz

    ins = (fk_in, pick_in, ccol_in, val_in, wk_in, fq_in, crow_in, wq_in)
    mine = (fk, pick, ccol, val, wk, fq, crow, wq)
    loads = [pltpu.make_async_copy(i, m, load.at[j]) for j, (i, m) in enumerate(zip(ins, mine))]
    for one in loads:
        one.start()

    def where_is(d):
        return {"wide": lax.div(d, narrow), "narrow": lax.rem(d, narrow)}

    def ahead(k):
        return lax.rem(me + k, n)

    barrier = pltpu.get_barrier_semaphore()

    @pl.loop(1, n)
    def _(k):
        pl.semaphore_signal(barrier, inc=1, device_id=where_is(ahead(k)), device_id_type=MESH)

    @pl.when(mz == 0)
    def _():
        upin[...] = jnp.zeros_like(upin)

    @pl.when(mz == narrow - 1)
    def _():
        downin[...] = jnp.zeros_like(downin)

    def cols(p):
        return pl.ds(pl.multiple_of(p * LANES, LANES), LANES)

    low = lax.broadcasted_iota(jnp.int32, (1, LANES), 1) < LANES // 2

    def piece(d):
        return pl.ds(pl.multiple_of(d * share, 8), share)

    def other(k):
        return lax.rem(mw + k, wide)

    def first(k):
        d = other(k)
        return pltpu.make_async_remote_copy(
            src_ref=state.at[piece(d), :], dst_ref=got.at[piece(mw), :],
            send_sem=send1.at[k], recv_sem=recv1.at[k],
            device_id={"wide": d, "narrow": mz}, device_id_type=MESH,
        )

    def second(i, sender):
        return pltpu.make_async_remote_copy(
            src_ref=scan.at[piece(i), :], dst_ref=prior.at[piece(mw), :],
            send_sem=send2.at[i], recv_sem=recv2.at[sender],
            device_id={"wide": i, "narrow": mz}, device_id_type=MESH,
        )

    def up(i):
        return pltpu.make_async_remote_copy(
            src_ref=upout.at[piece(i), :], dst_ref=upin.at[piece(i), :],
            send_sem=usend.at[i], recv_sem=urecv.at[i],
            device_id={"wide": mw, "narrow": lax.rem(mz + 1, narrow)}, device_id_type=MESH,
        )

    def down(i):
        return pltpu.make_async_remote_copy(
            src_ref=downout.at[piece(i), :], dst_ref=downin.at[piece(i), :],
            send_sem=dsend.at[i], recv_sem=drecv.at[i],
            device_id={"wide": mw, "narrow": lax.rem(mz + narrow - 1, narrow)}, device_id_type=MESH,
        )

    def rim(p, which):
        src, dst = ((wk, rimk), (val, rimv))[which]
        return pltpu.make_async_remote_copy(
            src_ref=src.at[:, cols(p)], dst_ref=dst.at[p],
            send_sem=rsend.at[which, p], recv_sem=rrecv.at[which, p],
            device_id=where_is(ahead(1)), device_id_type=MESH,
        )

    def rims(lo, hi):
        @pl.loop(lo, hi)
        def _(p):
            rim(p, 0).start()
            rim(p, 1).start()

    for one in loads[:5]:
        one.wait()
    pl.semaphore_wait(barrier, n - 1)
    rims(0, EARLY)

    if wide * share > pairs * padded:
        state[pl.ds(pairs * padded, wide * share - pairs * padded), :] = jnp.zeros(
            (wide * share - pairs * padded, LANES), F32
        )

    @pl.loop(0, pairs, unroll=4)
    def _(p):
        x = fk[:, cols(lax.div(2 * p, per))]
        v = val[:, cols(p)]
        base = pl.multiple_of(p * padded, 8)
        parts = []
        norms = []
        for e in range(2):
            j = lax.rem(2 * p + e, per)
            a = nt(pick[0, j], x) + ccol[:, 0:1]
            b = nt(pick[1, j], x) + ccol[:, 1:2]
            k = (a * b * ccol[:, 2:3]).astype(BF16)
            kft[2 * p + e] = k
            parts.append(nn(k, v))
            norms.append(nt(jnp.ones((8, rows), BF16), k))
        state[pl.ds(base, padded), :] = jnp.where(low, parts[0], parts[1])
        for e in range(2):
            state[pl.ds(base + feats + 2 * e, 1), :] = norms[e][0:1, 0:LANES]
            state[pl.ds(base + feats + 2 * e + 1, 1), 0 : padded - LANES] = norms[e][0:1, LANES:padded]

    @pl.loop(1, wide)
    def _(k):
        first(k).start()

    got[piece(mw), :] = state[piece(mw), :]
    for one in loads[5:]:
        one.wait()

    r = lax.broadcasted_iota(jnp.int32, (rows, rows), 0)
    c = lax.broadcasted_iota(jnp.int32, (rows, rows), 1)
    causal = r >= c

    @pl.loop(0, pairs, unroll=2)
    def _(p):
        x = fq[:, cols(lax.div(2 * p, per))]
        v = val[:, cols(p)]
        nums = []
        dens = []
        for e in range(2):
            j = lax.rem(2 * p + e, per)
            a = nt(x, pick[0, j]) + crow[0:1, :]
            b = nt(x, pick[1, j]) + crow[1:2, :]
            q = (a * b * crow[2:3, :]).astype(BF16)
            qf[2 * p + e] = q
            s = jnp.where(causal, nn(q, kft[2 * p + e]), F32(0.0))
            dens.append(jnp.sum(s, -1, keepdims=True))
            nums.append(nn(s.astype(BF16), v))
        num[:, cols(p)] = jnp.where(low, nums[0], nums[1])
        den[:, cols(p)] = jnp.where(low, dens[0], dens[1])

    @pl.loop(1, wide)
    def _(k):
        first(k).wait_recv()

    def add(d, total):
        scan[piece(d), :] = total
        total = total + got[piece(d), :]
        got[piece(d), :] = total
        return total

    lax.fori_loop(0, wide, add, jnp.zeros((share, LANES), F32))

    scale = BF16(1.0 / np.sqrt(LANES // 2))
    rim_ok = (c > r) & (me > 0)

    def attend(p):
        rim(p, 0).wait_recv()
        rim(p, 1).wait_recv()
        q = wq[:, cols(p)] * scale
        k = wk[:, cols(p)]
        v = val[:, cols(p)]
        rk = rimk[p]
        rv = rimv[p]
        outs = []
        for e in range(2):
            qe = jnp.where(low if e == 0 else ~low, q, jnp.zeros_like(q))
            s0 = jnp.where(rim_ok, nt(qe, rk), F32(-1e30))
            s1 = jnp.where(causal, nt(qe, k), F32(-1e30))
            m = jnp.maximum(jnp.max(s0, -1, keepdims=True), jnp.max(s1, -1, keepdims=True))
            e0 = jnp.exp(s0 - m)
            e1 = jnp.exp(s1 - m)
            inv = F32(1.0) / (jnp.sum(e0, -1, keepdims=True) + jnp.sum(e1, -1, keepdims=True))
            outs.append(nn((e0 * inv).astype(BF16), rv) + nn((e1 * inv).astype(BF16), v))
        window = jnp.where(low, outs[0], outs[1])

        held[:, cols(p)] = window

    lead = LAG * jnp.maximum(mz, narrow - 1 - mz)

    def slot(t):
        i = t - LAG * mz

        @pl.when((i >= 0) & (i < wide))
        def _():
            @pl.when(mz > 0)
            def _():
                up(i).wait_recv()

            @pl.when(mz < narrow - 1)
            def _():
                upout[piece(i), :] = upin[piece(i), :] + got[piece(i), :]
                up(i).start()

        j = t - LAG * (narrow - 1 - mz)

        @pl.when((j >= 0) & (j < wide))
        def _():
            @pl.when(mz < narrow - 1)
            def _():
                down(j).wait_recv()

            @pl.when(mz > 0)
            def _():
                downout[piece(j), :] = downin[piece(j), :] + scan[piece(j), :]
                down(j).start()

        o = t - lead

        @pl.when((o >= 0) & (o < wide))
        def _():
            scan[piece(o), :] = scan[piece(o), :] + upin[piece(o), :] + downin[piece(o), :]

            @pl.when(o == mw)
            def _():
                prior[piece(o), :] = scan[piece(o), :]

            @pl.when(o != mw)
            def _():
                second(o, mw).start()

    slots = wide + LAG * (narrow - 1)

    @pl.loop(0, slots)
    def _(t):
        slot(t)

        @pl.when(t < EARLY)
        def _():
            attend(t)

    rims(EARLY, pairs)

    @pl.loop(min(slots, EARLY), pairs)
    def _(p):
        attend(p)

    @pl.loop(1, wide)
    def _(k):
        second(other(k), other(k)).wait_recv()

    @pl.loop(0, pairs, unroll=4)
    def _(p):
        base = pl.multiple_of(p * padded, 8)
        tile = prior[pl.ds(base, padded), :]
        hi = tile.astype(BF16)
        rest = tile - hi.astype(F32)
        mid = rest.astype(BF16)
        lo = (rest - mid.astype(F32)).astype(BF16)
        crosses = []
        dens = []
        for e in range(2):
            qe = qf[2 * p + e]
            crosses.append(nn(qe, hi) + nn(qe, mid) + nn(qe, lo))
            at = feats + 2 * e
            z0 = tile[at : at + 1, :]
            z1 = tile[at + 1 : at + 2, 0 : padded - LANES]
            q32 = qe.astype(F32)
            dens.append(
                jnp.sum(q32[:, 0:LANES] * z0, -1, keepdims=True)
                + jnp.sum(q32[:, LANES:padded] * z1, -1, keepdims=True)
            )
        top = num[:, cols(p)] + jnp.where(low, crosses[0], crosses[1])
        bottom = den[:, cols(p)] + jnp.where(low, dens[0], dens[1])
        out[:, cols(p)] = (top / bottom + held[:, cols(p)]).astype(out.dtype)

    @pl.loop(1, wide)
    def _(k):
        first(k).wait_send()
        second(other(k), mw).wait_send()

    @pl.loop(0, wide)
    def _(i):
        @pl.when(mz < narrow - 1)
        def _():
            up(i).wait_send()

        @pl.when(mz > 0)
        def _():
            down(i).wait_send()

    @pl.loop(0, pairs)
    def _(p):
        rim(p, 0).wait_send()
        rim(p, 1).wait_send()


def solution(mesh):
    wide, narrow = mesh.shape["wide"], mesh.shape["narrow"]

    def body(feat_queries, feat_keys, values, window_queries, window_keys):
        rows, channels = values.shape
        assert rows == WINDOW and channels == HEADS * LANES // 2
        feats, padded, per, pick, extra = tables(feat_queries.shape[1] // HEADS)
        pairs = channels // LANES
        share = -(-pairs * padded // (8 * wide)) * 8
        whole = pltpu.VMEM((wide * share, LANES), F32)
        vmem = pl.BlockSpec(memory_space=pltpu.VMEM)
        ins = (
            feat_queries, feat_keys, values, window_queries, window_keys,
            jnp.asarray(pick, BF16), jnp.asarray(extra, F32), jnp.asarray(extra.T, F32),
        )
        return pl.pallas_call(
            functools.partial(kernel, (wide, narrow, feats, padded, per, share)),
            out_shape=jax.ShapeDtypeStruct((rows, channels), BF16),
            in_specs=[pl.BlockSpec(memory_space=pltpu.HBM)] * 8,
            out_specs=vmem,
            scratch_shapes=[
                *[pltpu.VMEM(one.shape, one.dtype) for one in ins],
                pltpu.VMEM((HEADS, rows, padded), BF16),
                pltpu.VMEM((HEADS, padded, rows), BF16),
                *[whole] * 8,
                pltpu.VMEM((pairs, rows, LANES), BF16),
                pltpu.VMEM((pairs, rows, LANES), BF16),
                pltpu.VMEM((rows, channels), F32),
                pltpu.VMEM((rows, channels), F32),
                pltpu.VMEM((rows, channels), F32),
                pltpu.SemaphoreType.DMA((8,)),
                *[pltpu.SemaphoreType.DMA((wide,))] * 8,
                pltpu.SemaphoreType.DMA((2, pairs)),
                pltpu.SemaphoreType.DMA((2, pairs)),
            ],
            compiler_params=pltpu.CompilerParams(
                collective_id=0, has_side_effects=True, vmem_limit_bytes=56 * 1024 * 1024
            ),
        )(*ins)

    spec = P(("wide", "narrow"), None)
    return jax.shard_map(
        body, mesh=mesh, in_specs=(spec,) * 5, out_specs=spec, check_vma=False
    )
```

profile of v0, /device:TPU:7, one launch (start us, length us, event | category | flops | bytes accessed | tf_op | source)
XLA Modules:
  0.0 62.2 jit_solution(17394163616377399249)
XLA Ops:
  0.0 60.3 %shard_map.82 = bf16[256,1024]{1,0:T(8,128)(2,1)} custom-call(bf16[256,256]{1,0:T(8,128)(2,1)} %fq_in.1, bf16[256,256]{1,0:T(8,128)(2,1)} %fk_in.1, bf16[256,1024]{1,0:T(8,128)(2,1)} %val_in.1, bf16[256,1024]{1,0:T(8,128)(2,1)} %wq_in.1, bf16[256,1024]{1,0:T(8,128)(2,1)} %wk_in.1, bf16[2,8,160,128]{3,2,1,0:T(8,128)(2,1)} %constant.6.clone.pick_in, ...), custom_call_target="tpu_custom_call" | custom-call | tf_op jit(solution)/shard_map/pallas_call | solution.py:373
  60.3 1.9 %copy.10 = bf16[256,1024]{1,0:T(8,128)(2,1)} copy(bf16[256,1024]{1,0:T(8,128)(2,1)} %shard_map.82) | data formatting | bytes 1048576
where the time goes:
time: 62.4 us; the launch traced here: 62.2 us
  Pallas kernels  60.3 us (97%)
  local copies, waits for them, and re-layouts  1.87 us (3%)
    pallas_call x1, Pallas kernels, body(): pl.pallas_call(functools.partial(kernel, (wide, narrow, feats, padded, pe...  60.3 us
    unnamed x1, local copies, waits for them, and re-layouts  1.87 us

commit v1 on v0

v1 whole, which is shorter than its diff:
```python
import functools

import jax
import jax.numpy as jnp
import numpy as np
from jax import lax
from jax.experimental import pallas as pl
from jax.experimental.pallas import tpu as pltpu
from jax.sharding import PartitionSpec as P

HEADS = 16
WINDOW = 256
LANES = 128
EARLY = 3
MORE = 1
AHEAD = 4
GROUP = 4
FAR = 6
PACE = 13
MIX = 2
RATE = 1
LAG = 2
FINE = 65000.0
MESH = pl.DeviceIdType.MESH
F32 = jnp.float32
BF16 = jnp.bfloat16
NT = (((1,), (1,)), ((), ()))


def nt(a, b):
    return lax.dot_general(a, b, NT, preferred_element_type=F32)


def nn(a, b):
    return jnp.dot(a, b, preferred_element_type=F32)


def layout(width):
    norms = 1 + 2 * width
    return norms, -(-(norms + 5) // 8) * 8


def tables(width):
    norms, plain = layout(width)
    pairs = [(i, i) for i in range(width)] + [(i, j) for i in range(width) for j in range(i + 1, width)]
    padded = plain + -(-(len(pairs) - width) // 24) * 24
    per = LANES // width
    one = np.zeros((padded, width))
    two = np.zeros((padded, width))
    extra = np.zeros((8, padded))
    extra[0, 0] = 1.0
    extra[1, : 1 + width] = 1.0
    extra[2, 0] = 1.0
    extra[2, 1 : 1 + width] = 1.0 / width**0.25
    for i in range(width):
        one[1 + i, i] = 1.0
    for n, (i, j) in enumerate(pairs):
        at = 1 + width + n if n < width else plain + n - width
        one[at, i] = 1.0
        two[at, j] = 1.0
        extra[2, at] = 1.0 / np.sqrt(2.0 * width) if i == j else 1.0 / np.sqrt(1.0 * width)
    pick = np.zeros((2, per, padded, LANES))
    for j in range(per):
        pick[0, j, :, j * width : (j + 1) * width] = one
        pick[1, j, :, j * width : (j + 1) * width] = two
    return padded, per, pick, extra


def kernel(
    dims,
    fq_in, fk_in, val_in, wq_in, wk_in, pick_in, crow_in, ccol_in,
    out,
    fq, fk, val, wq, wk, pick, crow, ccol,
    qf, kft, state, got, upin, upout, downin, downout, scan, prior, rimk, rimv, num, den, held,
    load, send1, recv1, send2, recv2, usend, urecv, dsend, drecv, rsend, rrecv,
):
    wide, narrow, padded, per, share = dims
    NORMS, PLAIN = layout(fq_in.shape[1] // HEADS)
    n = wide * narrow
    rows = val.shape[0]
    pairs = val.shape[1] // LANES
    chop = padded // share
    mw = lax.axis_index("wide")
    mz = lax.axis_index("narrow")
    me = mw * narrow + mz
    top_z = mz == narrow - 1
    not_last = me < n - 1

    ins = (fk_in, pick_in, ccol_in, val_in, fq_in, crow_in, wq_in, wk_in)
    mine = (fk, pick, ccol, val, fq, crow, wq, wk)
    loads = [pltpu.make_async_copy(i, m, load.at[j]) for j, (i, m) in enumerate(zip(ins, mine))]
    for one in loads:
        one.start()

    def where_is(d):
        return {"wide": lax.div(d, narrow), "narrow": lax.rem(d, narrow)}

    def other(k):
        return lax.rem(mw + k, wide)

    barrier = pltpu.get_barrier_semaphore()

    def greet(d):
        pl.semaphore_signal(barrier, inc=1, device_id=d, device_id_type=MESH)

    @pl.loop(1, wide)
    def _(k):
        greet({"wide": other(k), "narrow": mz})

    @pl.when(jnp.logical_not(top_z))
    def _():
        greet({"wide": mw, "narrow": mz + 1})

    @pl.when(mz > 0)
    def _():
        greet({"wide": mw, "narrow": mz - 1})

    @pl.when(top_z & not_last)
    def _():
        greet(where_is(me + 1))

    @pl.when((mz == 0) & (me > 0))
    def _():
        greet(where_is(me - 1))

    @pl.when(mz == 0)
    def _():
        upin[...] = jnp.zeros_like(upin)

    @pl.when(top_z)
    def _():
        downin[...] = jnp.zeros_like(downin)

    downin[pl.ds(0, upin.shape[0] // wide), :] = jnp.zeros((upin.shape[0] // wide, LANES), F32)

    @pl.when(me == 0)
    def _():
        rimk[...] = jnp.zeros_like(rimk)
        rimv[...] = jnp.zeros_like(rimv)

    def cols(p):
        return pl.ds(pl.multiple_of(p * LANES, LANES), LANES)

    low = lax.broadcasted_iota(jnp.int32, (1, LANES), 1) < LANES // 2

    def piece(d):
        return pl.ds(pl.multiple_of(d * share, 8), share)

    packed = share == padded
    size = upin.shape[0] // wide

    def note(i):
        return pl.ds(pl.multiple_of(i * size, 8), size)

    def write(ref, i, tile):
        if not packed:
            ref[note(i), :] = tile
            return
        third = (padded - PLAIN) // 3
        rest = tile[PLAIN:padded, :]
        most = jnp.maximum(jnp.max(jnp.abs(rest), 0, keepdims=True), F32(1e-30))
        fine = F32(FINE) / most
        one = jnp.floor(rest[0:third, :] * fine + F32(0.5))
        two = jnp.floor(rest[third : 2 * third, :] * (fine * F32(0.5)) + F32(0.5))
        three = jnp.floor(rest[2 * third :, :] * fine + F32(0.5))
        high = jnp.floor(two * F32(1.0 / 256.0))
        at = i * size
        ref[pl.ds(pl.multiple_of(at, 8), PLAIN), :] = tile[0:PLAIN, :]
        ref[pl.ds(at + PLAIN - 1, 1), :] = most
        ref[pl.ds(pl.multiple_of(at + PLAIN, 8), third), :] = one * F32(256.0) + (high + F32(128.0))
        ref[pl.ds(pl.multiple_of(at + PLAIN + third, 8), third), :] = three * F32(256.0) + (two - high * F32(256.0))

    def read(ref, i):
        if not packed:
            return ref[note(i), :]
        third = (padded - PLAIN) // 3
        at = i * size
        plain = ref[pl.ds(pl.multiple_of(at, 8), PLAIN), :]
        left = ref[pl.ds(pl.multiple_of(at + PLAIN, 8), third), :]
        right = ref[pl.ds(pl.multiple_of(at + PLAIN + third, 8), third), :]
        step = plain[PLAIN - 1 : PLAIN, :] * F32(1.0 / FINE)
        one = jnp.floor(left * F32(1.0 / 256.0))
        three = jnp.floor(right * F32(1.0 / 256.0))
        two = (left - one * F32(256.0) - F32(128.0)) * F32(256.0) + (right - three * F32(256.0))
        return jnp.concatenate([plain, one * step, two * (step * F32(2.0)), three * step], 0)

    def first(k):
        d = other(k)
        return pltpu.make_async_remote_copy(
            src_ref=state.at[piece(d), :], dst_ref=got.at[piece(mw), :],
            send_sem=send1.at[k], recv_sem=recv1.at[k],
            device_id={"wide": d, "narrow": mz}, device_id_type=MESH,
        )

    def second(i, sender):
        return pltpu.make_async_remote_copy(
            src_ref=scan.at[piece(i), :], dst_ref=prior.at[piece(mw), :],
            send_sem=send2.at[i], recv_sem=recv2.at[sender],
            device_id={"wide": i, "narrow": mz}, device_id_type=MESH,
        )

    def up(i):
        return pltpu.make_async_remote_copy(
            src_ref=upout.at[note(i), :], dst_ref=upin.at[note(i), :],
            send_sem=usend.at[i], recv_sem=urecv.at[i],
            device_id={"wide": mw, "narrow": lax.rem(mz + 1, narrow)}, device_id_type=MESH,
        )

    def down(i):
        return pltpu.make_async_remote_copy(
            src_ref=downout.at[note(i), :], dst_ref=downin.at[note(i), :],
            send_sem=dsend.at[i], recv_sem=drecv.at[i],
            device_id={"wide": mw, "narrow": lax.rem(mz + narrow - 1, narrow)}, device_id_type=MESH,
        )

    def rim(p, which):
        src, dst = ((wk_in, rimk), (val_in, rimv))[which]
        return pltpu.make_async_remote_copy(
            src_ref=src.at[:, cols(p)], dst_ref=dst.at[p],
            send_sem=rsend.at[which, p], recv_sem=rrecv.at[which, p],
            device_id=where_is(lax.rem(me + 1, n)), device_id_type=MESH,
        )

    def rims(lo, hi):
        @pl.when(not_last)
        def _():
            @pl.loop(lo, hi)
            def _(p):
                rim(p, 0).start()
                rim(p, 1).start()

    def early(z):
        return jnp.minimum(jnp.where(z == narrow - 1, 0, EARLY + MORE * z), pairs)

    far = jnp.where(lax.rem(mw, 2) == 0, FAR, 0)

    def keys(p):
        x = fk[:, cols(lax.div(2 * p, per))]
        v = val[:, cols(p)]
        base = pl.multiple_of(p * padded, 8)
        parts = []
        norms = []
        for e in range(2):
            j = lax.rem(2 * p + e, per)
            a = nt(pick[0, j], x) + ccol[:, 0:1]
            b = nt(pick[1, j], x) + ccol[:, 1:2]
            k = (a * b * ccol[:, 2:3]).astype(BF16)
            kft[2 * p + e] = k
            parts.append(nn(k, v))
            norms.append(nt(jnp.ones((8, rows), BF16), k))
        state[pl.ds(base, padded), :] = jnp.where(low, parts[0], parts[1])
        for e in range(2):
            state[pl.ds(base + NORMS + 2 * e, 1), :] = norms[e][0:1, 0:LANES]
            state[pl.ds(base + NORMS + 2 * e + 1, 1), 0 : padded - LANES] = norms[e][0:1, LANES:padded]

    def batch(g):
        return [lax.rem(lax.div(mw, chop) + 1 + g * GROUP + j, pairs) for j in range(GROUP)]

    def share_out(g):
        for p in batch(g):
            for e in range(chop):
                d = p * chop + e

                @pl.when(d != mw)
                def _():
                    first(lax.rem(d - mw + wide, wide)).start()

    for one in loads[:4]:
        one.wait()
    for p in batch(0):
        keys(p)
    pl.semaphore_wait(barrier, wide - 1 + (mz > 0) + jnp.logical_not(top_z) + (top_z & not_last) + ((mz == 0) & (me > 0)))
    share_out(0)
    rims(0, early(mz))

    @pl.when(top_z)
    def _():
        rims(0, far)

    @pl.loop(1, pairs // GROUP)
    def _(g):
        for p in batch(g):
            keys(p)
        share_out(g)

    got[piece(mw), :] = state[piece(mw), :]
    for one in loads[4:]:
        one.wait()

    r = lax.broadcasted_iota(jnp.int32, (rows, rows), 0)
    c = lax.broadcasted_iota(jnp.int32, (rows, rows), 1)
    causal = r >= c

    def intra(p):
        x = fq[:, cols(lax.div(2 * p, per))]
        v = val[:, cols(p)]
        nums = []
        dens = []
        for e in range(2):
            j = lax.rem(2 * p + e, per)
            a = nt(x, pick[0, j]) + crow[0:1, :]
            b = nt(x, pick[1, j]) + crow[1:2, :]
            q = (a * b * crow[2:3, :]).astype(BF16)
            qf[2 * p + e] = q
            s = jnp.where(causal, nn(q, kft[2 * p + e]), F32(0.0))
            dens.append(jnp.sum(s, -1, keepdims=True))
            nums.append(nn(s.astype(BF16), v))
        num[:, cols(p)] = jnp.where(low, nums[0], nums[1])
        den[:, cols(p)] = jnp.where(low, dens[0], dens[1])

    @pl.loop(0, AHEAD, unroll=2)
    def _(p):
        intra(p)

    @pl.loop(1, wide)
    def _(k):
        first(k).wait_recv()

    def add(d, total):
        scan[piece(d), :] = total
        total = total + got[piece(d), :]
        got[piece(d), :] = total
        return total

    lax.fori_loop(0, wide, add, jnp.zeros((share, LANES), F32))

    scale = BF16(1.0 / np.sqrt(LANES // 2))
    rim_ok = (c > r) & (me > 0)

    def attend(p):
        @pl.when(me > 0)
        def _():
            rim(p, 0).wait_recv()
            rim(p, 1).wait_recv()

        q = wq[:, cols(p)] * scale
        k = wk[:, cols(p)]
        v = val[:, cols(p)]
        rk = rimk[p]
        rv = rimv[p]
        outs = []
        for e in range(2):
            qe = jnp.where(low if e == 0 else ~low, q, jnp.zeros_like(q))
            s0 = jnp.where(rim_ok, nt(qe, rk), F32(-1e30))
            s1 = jnp.where(causal, nt(qe, k), F32(-1e30))
            m = jnp.maximum(jnp.max(s0, -1, keepdims=True), jnp.max(s1, -1, keepdims=True))
            e0 = jnp.exp(s0 - m)
            e1 = jnp.exp(s1 - m)
            inv = F32(1.0) / (jnp.sum(e0, -1, keepdims=True) + jnp.sum(e1, -1, keepdims=True))
            outs.append(nn((e0 * inv).astype(BF16), rv) + nn((e1 * inv).astype(BF16), v))
        return jnp.where(low, outs[0], outs[1])

    lead = LAG * jnp.maximum(mz, narrow - 1 - mz)
    spent = wide - 1 + LAG * mz

    @pl.when(mz == 0)
    def _():
        @pl.loop(0, wide)
        def _(i):
            write(upout, i, got[piece(i), :])
            up(i).start()

        rims(early(mz), pairs)

    @pl.when(top_z)
    def _():
        @pl.loop(1, wide)
        def _(j):
            write(downout, j, scan[piece(j), :])
            down(j).start()

    def slot(t):
        i = t - LAG * mz

        @pl.when((i >= 0) & (i < wide) & (mz > 0))
        def _():
            up(i).wait_recv()

            @pl.when(mz < narrow - 1)
            def _():
                write(upout, i, read(upin, i) + got[piece(i), :])
                up(i).start()

        j = t - LAG * (narrow - 1 - mz)

        @pl.when((j >= 1) & (j < wide) & (mz < narrow - 1))
        def _():
            down(j).wait_recv()

            @pl.when(mz > 0)
            def _():
                write(downout, j, read(downin, j) + scan[piece(j), :])
                down(j).start()

        o = t - lead

        @pl.when((o >= 0) & (o < wide))
        def _():
            scan[piece(o), :] = scan[piece(o), :] + read(upin, o) + read(downin, o)

            @pl.when(o == mw)
            def _():
                prior[piece(o), :] = scan[piece(o), :]

            @pl.when(o != mw)
            def _():
                second(o, mw).start()

        @pl.when((t == spent) & (mz > 0) & (mz < narrow - 1))
        def _():
            rims(early(mz), pairs)

        @pl.when(top_z & (t == PACE))
        def _():
            rims(far, pairs)

    slots = wide + LAG * (narrow - 1)
    rest = pairs - AHEAD
    due = jnp.where(mz > 0, early(mz - 1), jnp.where(lax.rem(mw, 2) == 1, FAR, 0))
    done = jnp.minimum(due, slots - rest)

    @pl.loop(0, slots)
    def _(t):
        slot(t)

        @pl.when(t < rest)
        def _():
            intra(AHEAD + t)

        @pl.when((t >= rest) & (t - rest < done))
        def _():
            held[:, cols(t - rest)] = attend(t - rest)

    @pl.loop(1, wide)
    def _(k):
        second(other(k), other(k)).wait_recv()

    @pl.loop(0, pairs, unroll=4)
    def _(p):
        base = pl.multiple_of(p * padded, 8)
        tile = prior[pl.ds(base, padded), :]
        hi = tile.astype(BF16)
        mid = (tile - hi.astype(F32)).astype(BF16)
        crosses = []
        dens = []
        for e in range(2):
            qe = qf[2 * p + e]
            crosses.append(nn(qe, hi) + nn(qe, mid))
            at = NORMS + 2 * e
            z0 = tile[at : at + 1, :]
            z1 = tile[at + 1 : at + 2, 0 : padded - LANES]
            q32 = qe.astype(F32)
            dens.append(
                jnp.sum(q32[:, 0:LANES] * z0, -1, keepdims=True)
                + jnp.sum(q32[:, LANES:padded] * z1, -1, keepdims=True)
            )
        top = num[:, cols(p)] + jnp.where(low, crosses[0], crosses[1])
        bottom = den[:, cols(p)] + jnp.where(low, dens[0], dens[1])
        num[:, cols(p)] = top / bottom

    @pl.loop(0, done)
    def _(p):
        out[:, cols(p)] = (num[:, cols(p)] + held[:, cols(p)]).astype(out.dtype)

    @pl.loop(done, pairs)
    def _(p):
        out[:, cols(p)] = (num[:, cols(p)] + attend(p)).astype(out.dtype)

    @pl.loop(1, wide)
    def _(k):
        first(k).wait_send()
        second(other(k), mw).wait_send()

    @pl.loop(0, wide)
    def _(i):
        @pl.when(mz < narrow - 1)
        def _():
            up(i).wait_send()

        @pl.when((mz > 0) & (i > 0))
        def _():
            down(i).wait_send()

    @pl.when(not_last)
    def _():
        @pl.loop(0, pairs)
        def _(p):
            rim(p, 0).wait_send()
            rim(p, 1).wait_send()


def solution(mesh):
    wide, narrow = mesh.shape["wide"], mesh.shape["narrow"]

    def body(feat_queries, feat_keys, values, window_queries, window_keys):
        rows, channels = values.shape
        assert rows == WINDOW and channels == HEADS * LANES // 2
        padded, per, pick, extra = tables(feat_queries.shape[1] // HEADS)
        pairs = channels // LANES
        share = -(-pairs * padded // (8 * wide)) * 8
        whole = pltpu.VMEM((wide * share, LANES), F32)
        plain = layout(feat_queries.shape[1] // HEADS)[1]
        size = plain + (padded - plain) // 3 * 2 if share == padded else share
        notes = pltpu.VMEM((wide * size, LANES), F32)
        assert padded % share == 0
        vmem = pl.BlockSpec(memory_space=pltpu.VMEM)
        ins = (
            feat_queries, feat_keys, values, window_queries, window_keys,
            jnp.asarray(pick, BF16), jnp.asarray(extra, F32), jnp.asarray(extra.T, F32),
        )
        return pl.pallas_call(
            functools.partial(kernel, (wide, narrow, padded, per, share)),
            out_shape=jax.ShapeDtypeStruct((rows, channels), BF16),
            in_specs=[pl.BlockSpec(memory_space=pltpu.HBM)] * 8,
            out_specs=vmem,
            scratch_shapes=[
                *[pltpu.VMEM(one.shape, one.dtype) for one in ins],
                pltpu.VMEM((HEADS, rows, padded), BF16),
                pltpu.VMEM((HEADS, padded, rows), BF16),
                *[whole] * 2,
                *[notes] * 4,
                *[whole] * 2,
                pltpu.VMEM((pairs, rows, LANES), BF16),
                pltpu.VMEM((pairs, rows, LANES), BF16),
                pltpu.VMEM((rows, channels), F32),
                pltpu.VMEM((rows, channels), F32),
                pltpu.VMEM((rows, channels), F32),
                pltpu.SemaphoreType.DMA((8,)),
                *[pltpu.SemaphoreType.DMA((wide,))] * 8,
                pltpu.SemaphoreType.DMA((2, pairs)),
                pltpu.SemaphoreType.DMA((2, pairs)),
            ],
            compiler_params=pltpu.CompilerParams(
                collective_id=0, has_side_effects=True, vmem_limit_bytes=56 * 1024 * 1024
            ),
        )(*ins)

    spec = P(("wide", "narrow"), None)
    return jax.shard_map(
        body, mesh=mesh, in_specs=(spec,) * 5, out_specs=spec, check_vma=False
    )
```

time: 62.4 us -> 55 us (0.88)
  the two profiles are of different devices: /device:TPU:7 before, /device:TPU:4 now
where the time goes in v1:
time: 55 us; the launch traced here: 54.8 us
  Pallas kernels  52.9 us (96%)
  local copies, waits for them, and re-layouts  1.87 us (3%)
    pallas_call x1, Pallas kernels, body(): pl.pallas_call(functools.partial(kernel, (wide, narrow, padded, per, shar...  52.9 us
    unnamed x1, local copies, waits for them, and re-layouts  1.87 us

profile of v1, /device:TPU:4, one launch (start us, length us, event | category | flops | bytes accessed | tf_op | source)
XLA Modules:
  0.0 54.8 jit_solution(11336727074628044972)
XLA Ops:
  0.0 52.9 %shard_map.82 = bf16[256,1024]{1,0:T(8,128)(2,1)} custom-call(bf16[256,256]{1,0:T(8,128)(2,1)} %fq_in.1, bf16[256,256]{1,0:T(8,128)(2,1)} %fk_in.1, bf16[256,1024]{1,0:T(8,128)(2,1)} %val_in.1, bf16[256,1024]{1,0:T(8,128)(2,1)} %wq_in.1, bf16[256,1024]{1,0:T(8,128)(2,1)} %wk_in.1, bf16[2,8,160,128]{3,2,1,0:T(8,128)(2,1)} %constant.6.clone.pick_in, ...), custom_call_target="tpu_custom_call" | custom-call | tf_op jit(solution)/shard_map/pallas_call | solution.py:511
  52.9 1.9 %copy.10 = bf16[256,1024]{1,0:T(8,128)(2,1)} copy(bf16[256,1024]{1,0:T(8,128)(2,1)} %shard_map.82) | data formatting | bytes 1048576

commit v2 on v1

--- a/solution.py
+++ b/solution.py
@@ -11,13 +11,15 @@
 HEADS = 16
 WINDOW = 256
 LANES = 128
-EARLY = 3
+EARLY = 2
 MORE = 1
 AHEAD = 4
-GROUP = 4
-FAR = 6
-PACE = 13
-MIX = 2
+GROUP = 2
+FAR = 5
+PACE = 10
+MIX = 0
+STEP = 1
+BURST = 1
 RATE = 1
 LAG = 2
 FINE = 65000.0
@@ -71,8 +73,9 @@
     fq_in, fk_in, val_in, wq_in, wk_in, pick_in, crow_in, ccol_in,
     out,
     fq, fk, val, wq, wk, pick, crow, ccol,
-    qf, kft, state, got, upin, upout, downin, downout, scan, prior, rimk, rimv, num, den, held,
-    load, send1, recv1, send2, recv2, usend, urecv, dsend, drecv, rsend, rrecv,
+    qf, kft, own, scan, state, got, upin, upout, downin, downout, base, prior,
+    rimk, rimv, farsk, farsv, num, den, held,
+    load, send1, recv1, send2, recv2, usend, urecv, dsend, drecv, rsend, rrecv, hrecv, psend,
 ):
     wide, narrow, padded, per, share = dims
     NORMS, PLAIN = layout(fq_in.shape[1] // HEADS)
@@ -115,13 +118,23 @@
     def _():
         greet({"wide": mw, "narrow": mz - 1})
 
-    @pl.when(top_z & not_last)
-    def _():
-        greet(where_is(me + 1))
-
-    @pl.when((mz == 0) & (me > 0))
-    def _():
-        greet(where_is(me - 1))
+    even = lax.rem(mw, 2) == 0
+    ahead_of = top_z & even & (mw < wide - 1)
+    passes = top_z & even & (mw > 0)
+    hands = top_z & jnp.logical_not(even) & (mw < wide - 1)
+    plain_rim = not_last & jnp.logical_not(hands)
+
+    @pl.when(ahead_of)
+    def _():
+        greet({"wide": mw + 1, "narrow": 0})
+
+    @pl.when(passes)
+    def _():
+        greet({"wide": mw, "narrow": 0})
+
+    @pl.when((mz == 0) & (mw > 0))
+    def _():
+        greet({"wide": jnp.where(even, mw, mw - 1), "narrow": narrow - 1})
 
     @pl.when(mz == 0)
     def _():
@@ -187,14 +200,14 @@
     def first(k):
         d = other(k)
         return pltpu.make_async_remote_copy(
-            src_ref=state.at[piece(d), :], dst_ref=got.at[piece(mw), :],
+            src_ref=state.at[note(d), :], dst_ref=got.at[note(mw), :],
             send_sem=send1.at[k], recv_sem=recv1.at[k],
             device_id={"wide": d, "narrow": mz}, device_id_type=MESH,
         )
 
     def second(i, sender):
         return pltpu.make_async_remote_copy(
-            src_ref=scan.at[piece(i), :], dst_ref=prior.at[piece(mw), :],
+            src_ref=base.at[note(i), :], dst_ref=prior.at[note(mw), :],
             send_sem=send2.at[i], recv_sem=recv2.at[sender],
             device_id={"wide": i, "narrow": mz}, device_id_type=MESH,
         )
@@ -221,8 +234,24 @@
             device_id=where_is(lax.rem(me + 1, n)), device_id_type=MESH,
         )
 
+    def hand(p, which):
+        src, dst = ((wk_in, farsk), (val_in, farsv))[which]
+        return pltpu.make_async_remote_copy(
+            src_ref=src.at[:, cols(p)], dst_ref=dst.at[p],
+            send_sem=rsend.at[which, p], recv_sem=hrecv.at[which, p],
+            device_id={"wide": other(1), "narrow": mz}, device_id_type=MESH,
+        )
+
+    def relay(p, which):
+        src, dst = ((farsk, rimk), (farsv, rimv))[which]
+        return pltpu.make_async_remote_copy(
+            src_ref=src.at[p], dst_ref=dst.at[p],
+            send_sem=psend.at[which, p], recv_sem=rrecv.at[which, p],
+            device_id={"wide": mw, "narrow": 0}, device_id_type=MESH,
+        )
+
     def rims(lo, hi):
-        @pl.when(not_last)
+        @pl.when(plain_rim)
         def _():
             @pl.loop(lo, hi)
             def _(p):
@@ -237,7 +266,7 @@
     def keys(p):
         x = fk[:, cols(lax.div(2 * p, per))]
         v = val[:, cols(p)]
-        base = pl.multiple_of(p * padded, 8)
+        at = pl.multiple_of(p * padded, 8)
         parts = []
         norms = []
         for e in range(2):
@@ -248,10 +277,12 @@
             kft[2 * p + e] = k
             parts.append(nn(k, v))
             norms.append(nt(jnp.ones((8, rows), BF16), k))
-        state[pl.ds(base, padded), :] = jnp.where(low, parts[0], parts[1])
+        own[pl.ds(at, padded), :] = jnp.where(low, parts[0], parts[1])
         for e in range(2):
-            state[pl.ds(base + NORMS + 2 * e, 1), :] = norms[e][0:1, 0:LANES]
-            state[pl.ds(base + NORMS + 2 * e + 1, 1), 0 : padded - LANES] = norms[e][0:1, LANES:padded]
+            own[pl.ds(at + NORMS + 2 * e, 1), :] = norms[e][0:1, 0:LANES]
+            own[pl.ds(at + NORMS + 2 * e + 1, 1), 0 : padded - LANES] = norms[e][0:1, LANES:padded]
+        for e in range(chop):
+            write(state, p * chop + e, own[piece(p * chop + e), :])
 
     def batch(g):
         return [lax.rem(lax.div(mw, chop) + 1 + g * GROUP + j, pairs) for j in range(GROUP)]
@@ -269,7 +300,7 @@
         one.wait()
     for p in batch(0):
         keys(p)
-    pl.semaphore_wait(barrier, wide - 1 + (mz > 0) + jnp.logical_not(top_z) + (top_z & not_last) + ((mz == 0) & (me > 0)))
+    pl.semaphore_wait(barrier, wide - 1 + (mz > 0) + jnp.logical_not(top_z) + ahead_of + passes + ((mz == 0) & (mw > 0)))
     share_out(0)
     rims(0, early(mz))
 
@@ -283,7 +314,6 @@
             keys(p)
         share_out(g)
 
-    got[piece(mw), :] = state[piece(mw), :]
     for one in loads[4:]:
         one.wait()
 
@@ -316,10 +346,12 @@
     def _(k):
         first(k).wait_recv()
 
+    mine_tile = own[piece(mw), :]
+
     def add(d, total):
         scan[piece(d), :] = total
-        total = total + got[piece(d), :]
-        got[piece(d), :] = total
+        total = total + jnp.where(d == mw, mine_tile, read(got, d))
+        own[piece(d), :] = total
         return total
 
     lax.fori_loop(0, wide, add, jnp.zeros((share, LANES), F32))
@@ -357,19 +389,55 @@
     def _():
         @pl.loop(0, wide)
         def _(i):
-            write(upout, i, got[piece(i), :])
+            write(upout, i, own[piece(i), :])
             up(i).start()
 
         rims(early(mz), pairs)
 
-    @pl.when(top_z)
-    def _():
-        @pl.loop(1, wide)
-        def _(j):
-            write(downout, j, scan[piece(j), :])
-            down(j).start()
+    @pl.when(hands)
+    def _():
+        @pl.loop(0, pairs)
+        def _(p):
+            hand(p, 0).start()
+            hand(p, 1).start()
+
+
+    left = 2 * (pairs - FAR)
+    mixed = (wide - 1 - MIX) * BURST
+
+    def either(make, q, act):
+        for which in range(2):
+
+            @pl.when(lax.rem(q, 2) == which)
+            def _():
+                act(make(lax.div(q, 2), which))
+
+    def flow(q):
+        @pl.when(ahead_of & (q < left))
+        def _():
+            either(rim, 2 * FAR + q, lambda copy: copy.start())
+
+        @pl.when(passes & (q >= left) & (q < left + 2 * pairs))
+        def _():
+            either(hand, q - left, lambda copy: copy.wait_recv())
+            either(relay, q - left, lambda copy: copy.start())
 
     def slot(t):
+        @pl.when(top_z & (t < wide - 1))
+        def _():
+            write(downout, t + 1, scan[piece(t + 1), :])
+            down(t + 1).start()
+
+            @pl.when(even & (t >= MIX))
+            def _():
+                for e in range(BURST):
+                    flow((t - MIX) * BURST + e)
+
+        @pl.when(top_z & even & (t >= PACE) & (lax.rem(t - PACE, STEP) == 0))
+        def _():
+            for e in range(RATE):
+                flow(mixed + lax.div(t - PACE, STEP) * RATE + e)
+
         i = t - LAG * mz
 
         @pl.when((i >= 0) & (i < wide) & (mz > 0))
@@ -378,7 +446,7 @@
 
             @pl.when(mz < narrow - 1)
             def _():
-                write(upout, i, read(upin, i) + got[piece(i), :])
+                write(upout, i, read(upin, i) + own[piece(i), :])
                 up(i).start()
 
         j = t - LAG * (narrow - 1 - mz)
@@ -396,23 +464,20 @@
 
         @pl.when((o >= 0) & (o < wide))
         def _():
-            scan[piece(o), :] = scan[piece(o), :] + read(upin, o) + read(downin, o)
+            tile = scan[piece(o), :] + read(upin, o) + read(downin, o)
 
             @pl.when(o == mw)
             def _():
-                prior[piece(o), :] = scan[piece(o), :]
+                write(prior, o, tile)
 
             @pl.when(o != mw)
             def _():
+                write(base, o, tile)
                 second(o, mw).start()
 
         @pl.when((t == spent) & (mz > 0) & (mz < narrow - 1))
         def _():
             rims(early(mz), pairs)
-
-        @pl.when(top_z & (t == PACE))
-        def _():
-            rims(far, pairs)
 
     slots = wide + LAG * (narrow - 1)
     rest = pairs - AHEAD
@@ -431,14 +496,19 @@
         def _():
             held[:, cols(t - rest)] = attend(t - rest)
 
+    @pl.when(top_z & even)
+    def _():
+        @pl.loop(mixed + max(0, -(-(slots - PACE) // STEP)) * RATE, left + 2 * pairs)
+        def _(q):
+            flow(q)
+
     @pl.loop(1, wide)
     def _(k):
         second(other(k), other(k)).wait_recv()
 
     @pl.loop(0, pairs, unroll=4)
     def _(p):
-        base = pl.multiple_of(p * padded, 8)
-        tile = prior[pl.ds(base, padded), :]
+        tile = jnp.concatenate([read(prior, p * chop + e) for e in range(chop)], 0)
         hi = tile.astype(BF16)
         mid = (tile - hi.astype(F32)).astype(BF16)
         crosses = []
@@ -462,10 +532,6 @@
     def _(p):
         out[:, cols(p)] = (num[:, cols(p)] + held[:, cols(p)]).astype(out.dtype)
 
-    @pl.loop(done, pairs)
-    def _(p):
-        out[:, cols(p)] = (num[:, cols(p)] + attend(p)).astype(out.dtype)
-
     @pl.loop(1, wide)
     def _(k):
         first(k).wait_send()
@@ -481,12 +547,23 @@
         def _():
             down(i).wait_send()
 
+    @pl.loop(done, pairs)
+    def _(p):
+        out[:, cols(p)] = (num[:, cols(p)] + attend(p)).astype(out.dtype)
+
     @pl.when(not_last)
     def _():
         @pl.loop(0, pairs)
         def _(p):
             rim(p, 0).wait_send()
             rim(p, 1).wait_send()
+
+    @pl.when(passes)
+    def _():
+        @pl.loop(0, pairs)
+        def _(p):
+            relay(p, 0).wait_send()
+            relay(p, 1).wait_send()
 
 
 def solution(mesh):
@@ -503,35 +580,30 @@
         size = plain + (padded - plain) // 3 * 2 if share == padded else share
         notes = pltpu.VMEM((wide * size, LANES), F32)
         assert padded % share == 0
-        vmem = pl.BlockSpec(memory_space=pltpu.VMEM)
         ins = (
             feat_queries, feat_keys, values, window_queries, window_keys,
             jnp.asarray(pick, BF16), jnp.asarray(extra, F32), jnp.asarray(extra.T, F32),
         )
+        ins = tuple(pltpu.with_memory_space_constraint(one, pltpu.HBM) for one in ins)
         return pl.pallas_call(
             functools.partial(kernel, (wide, narrow, padded, per, share)),
             out_shape=jax.ShapeDtypeStruct((rows, channels), BF16),
             in_specs=[pl.BlockSpec(memory_space=pltpu.HBM)] * 8,
-            out_specs=vmem,
+            out_specs=pl.BlockSpec(memory_space=pltpu.VMEM),
             scratch_shapes=[
                 *[pltpu.VMEM(one.shape, one.dtype) for one in ins],
                 pltpu.VMEM((HEADS, rows, padded), BF16),
                 pltpu.VMEM((HEADS, padded, rows), BF16),
                 *[whole] * 2,
-                *[notes] * 4,
-                *[whole] * 2,
-                pltpu.VMEM((pairs, rows, LANES), BF16),
-                pltpu.VMEM((pairs, rows, LANES), BF16),
-                pltpu.VMEM((rows, channels), F32),
-                pltpu.VMEM((rows, channels), F32),
-                pltpu.VMEM((rows, channels), F32),
+                *[notes] * 8,
+                *[pltpu.VMEM((pairs, rows, LANES), BF16)] * 4,
+                *[pltpu.VMEM((rows, channels), F32)] * 3,
                 pltpu.SemaphoreType.DMA((8,)),
                 *[pltpu.SemaphoreType.DMA((wide,))] * 8,
-                pltpu.SemaphoreType.DMA((2, pairs)),
-                pltpu.SemaphoreType.DMA((2, pairs)),
+                *[pltpu.SemaphoreType.DMA((2, pairs))] * 4,
             ],
             compiler_params=pltpu.CompilerParams(
-                collective_id=0, has_side_effects=True, vmem_limit_bytes=56 * 1024 * 1024
+                collective_id=0, has_side_effects=True, vmem_limit_bytes=40 * 1024 * 1024
             ),
         )(*ins)
 

time: 55 us -> 51.2 us (0.931)
  Pallas kernels: 52.9 us -> 50.1 us
  local copies, waits for them, and re-layouts: 1.87 us -> 0.8 us
    pallas_call x1, Pallas kernels: 52.9 us -> 50.1 us  [body(): pl.pallas_call(functools.partial(kernel, (wide, narrow, padded, per, shar...]
    unnamed x1, local copies, waits for them, and re-layouts: 1.87 us -> 0.8 us
where the time goes in v2:
time: 51.2 us; the launch traced here: 50.9 us
  Pallas kernels  50.1 us (98%)
  local copies, waits for them, and re-layouts  0.8 us (2%)
    pallas_call x1, Pallas kernels, body(): pl.pallas_call(functools.partial(kernel, (wide, narrow, padded, per, shar...  50.1 us

profile of v2, /device:TPU:4, one launch (start us, length us, event | category | flops | bytes accessed | tf_op | source)
XLA Modules:
  0.0 50.9 jit_solution(11488327503719803748)
XLA Ops:
  0.0 50.1 %shard_map.82 = bf16[256,1024]{1,0:T(8,128)(2,1)S(1)} custom-call(bf16[256,256]{1,0:T(8,128)(2,1)} %fq_in.1, bf16[256,256]{1,0:T(8,128)(2,1)} %fk_in.1, bf16[256,1024]{1,0:T(8,128)(2,1)} %val_in.1, bf16[256,1024]{1,0:T(8,128)(2,1)} %wq_in.1, bf16[256,1024]{1,0:T(8,128)(2,1)} %wk_in.1, bf16[2,8,160,128]{3,2,1,0:T(8,128)(2,1)} %constant.6.clone.pick_in, ...), custom_call_target="tpu_custom_call" | custom-call | tf_op jit(solution)/shard_map/pallas_call | solution.py:588
  50.1 0.8 %copy.10 = bf16[256,1024]{1,0:T(8,128)(2,1)} copy(bf16[256,1024]{1,0:T(8,128)(2,1)S(1)} %shard_map.82) | data formatting | bytes 1048576

commit v3 on v2

--- a/solution.py
+++ b/solution.py
@@ -16,12 +16,15 @@
 AHEAD = 4
 GROUP = 2
 FAR = 5
-PACE = 10
+PACE = 9
 MIX = 0
 STEP = 1
 BURST = 1
 RATE = 1
 LAG = 2
+FIRST = 2
+DIRECT = 5
+KEEP = 0
 FINE = 65000.0
 MESH = pl.DeviceIdType.MESH
 F32 = jnp.float32
@@ -74,7 +77,7 @@
     out,
     fq, fk, val, wq, wk, pick, crow, ccol,
     qf, kft, own, scan, state, got, upin, upout, downin, downout, base, prior,
-    rimk, rimv, farsk, farsv, num, den, held,
+    rimk, rimv, farsk, farsv, num, den, held, expo, peak, mass,
     load, send1, recv1, send2, recv2, usend, urecv, dsend, drecv, rsend, rrecv, hrecv, psend,
 ):
     wide, narrow, padded, per, share = dims
@@ -123,6 +126,19 @@
     passes = top_z & even & (mw > 0)
     hands = top_z & jnp.logical_not(even) & (mw < wide - 1)
     plain_rim = not_last & jnp.logical_not(hands)
+    columns = max(wide // 2, 1)
+
+    def relayed(w):
+        return pairs - lax.div(max(pairs - KEEP, 0) * jnp.maximum(columns - 1 - lax.div(w, 2), 0), columns)
+
+    @pl.when(hands)
+    def _():
+        greet(where_is(me + 1))
+
+    @pl.when((mz == 0) & even & (mw > 0))
+    def _():
+        greet(where_is(me - 1))
+
 
     @pl.when(ahead_of)
     def _():
@@ -300,7 +316,7 @@
         one.wait()
     for p in batch(0):
         keys(p)
-    pl.semaphore_wait(barrier, wide - 1 + (mz > 0) + jnp.logical_not(top_z) + ahead_of + passes + ((mz == 0) & (mw > 0)))
+    pl.semaphore_wait(barrier, wide - 1 + (mz > 0) + jnp.logical_not(top_z) + ahead_of + passes + hands + ((mz == 0) & (mw > 0)) + ((mz == 0) & even & (mw > 0)))
     share_out(0)
     rims(0, early(mz))
 
@@ -382,6 +398,43 @@
             outs.append(nn((e0 * inv).astype(BF16), rv) + nn((e1 * inv).astype(BF16), v))
         return jnp.where(low, outs[0], outs[1])
 
+    def part(p, e):
+        q = wq[:, cols(p)] * scale
+        return jnp.where(low if e == 0 else ~low, q, jnp.zeros_like(q))
+
+    def begin(p):
+        k = wk[:, cols(p)]
+        for e in range(2):
+            s1 = jnp.where(causal, nt(part(p, e), k), F32(-1e30))
+            m = jnp.max(s1, -1, keepdims=True)
+            e1 = jnp.exp(s1 - m)
+            expo[2 * p + e] = e1
+            peak[2 * p + e] = jnp.broadcast_to(m, (rows, LANES))
+            mass[2 * p + e] = jnp.broadcast_to(jnp.sum(e1, -1, keepdims=True), (rows, LANES))
+
+    def finish(p):
+        @pl.when(me > 0)
+        def _():
+            rim(p, 0).wait_recv()
+            rim(p, 1).wait_recv()
+
+        v = val[:, cols(p)]
+        rk = rimk[p]
+        rv = rimv[p]
+        outs = []
+        for e in range(2):
+            s0 = jnp.where(rim_ok, nt(part(p, e), rk), F32(-1e30))
+            m1 = peak[2 * p + e]
+            m = jnp.maximum(jnp.max(s0, -1, keepdims=True), m1)
+            halves = [jnp.exp(s0[:, n : n + LANES] - m) for n in range(0, rows, LANES)]
+            c1 = jnp.exp(m1 - m)
+            inv = F32(1.0) / (jnp.sum(sum(halves), -1, keepdims=True) + mass[2 * p + e] * c1)
+            c1 = c1 * inv
+            w1 = jnp.concatenate([(expo[2 * p + e][:, n : n + LANES] * c1).astype(BF16) for n in range(0, rows, LANES)], 1)
+            w0 = jnp.concatenate([(one * inv).astype(BF16) for one in halves], 1)
+            outs.append(nn(w1, v) + nn(w0, rv))
+        return jnp.where(low, outs[0], outs[1])
+
     lead = LAG * jnp.maximum(mz, narrow - 1 - mz)
     spent = wide - 1 + LAG * mz
 
@@ -396,7 +449,7 @@
 
     @pl.when(hands)
     def _():
-        @pl.loop(0, pairs)
+        @pl.loop(0, relayed(mw))
         def _(p):
             hand(p, 0).start()
             hand(p, 1).start()
@@ -417,7 +470,7 @@
         def _():
             either(rim, 2 * FAR + q, lambda copy: copy.start())
 
-        @pl.when(passes & (q >= left) & (q < left + 2 * pairs))
+        @pl.when(passes & (q >= left) & (q < left + 2 * relayed(mw - 1)))
         def _():
             either(hand, q - left, lambda copy: copy.wait_recv())
             either(relay, q - left, lambda copy: copy.start())
@@ -496,11 +549,25 @@
         def _():
             held[:, cols(t - rest)] = attend(t - rest)
 
+        @pl.when((t - rest >= done) & (t - rest < pairs))
+        def _():
+            begin(t - rest)
+
+    @pl.loop(jnp.maximum(slots - rest, done), pairs)
+    def _(p):
+        begin(p)
+
     @pl.when(top_z & even)
     def _():
         @pl.loop(mixed + max(0, -(-(slots - PACE) // STEP)) * RATE, left + 2 * pairs)
         def _(q):
             flow(q)
+
+    soon = done + jnp.where((mz == 0) & even, FIRST, 0)
+
+    @pl.loop(done, soon)
+    def _(p):
+        held[:, cols(p)] = finish(p)
 
     @pl.loop(1, wide)
     def _(k):
@@ -528,7 +595,7 @@
         bottom = den[:, cols(p)] + jnp.where(low, dens[0], dens[1])
         num[:, cols(p)] = top / bottom
 
-    @pl.loop(0, done)
+    @pl.loop(0, soon)
     def _(p):
         out[:, cols(p)] = (num[:, cols(p)] + held[:, cols(p)]).astype(out.dtype)
 
@@ -547,9 +614,22 @@
         def _():
             down(i).wait_send()
 
-    @pl.loop(done, pairs)
+    turn = jnp.clip(DIRECT, soon, pairs)
+
+    @pl.loop(soon, turn)
     def _(p):
-        out[:, cols(p)] = (num[:, cols(p)] + attend(p)).astype(out.dtype)
+        out[:, cols(p)] = (num[:, cols(p)] + finish(p)).astype(out.dtype)
+
+    @pl.when(hands)
+    def _():
+        @pl.loop(relayed(mw), pairs)
+        def _(p):
+            rim(p, 0).start()
+            rim(p, 1).start()
+
+    @pl.loop(turn, pairs)
+    def _(p):
+        out[:, cols(p)] = (num[:, cols(p)] + finish(p)).astype(out.dtype)
 
     @pl.when(not_last)
     def _():
@@ -560,7 +640,7 @@
 
     @pl.when(passes)
     def _():
-        @pl.loop(0, pairs)
+        @pl.loop(0, relayed(mw - 1))
         def _(p):
             relay(p, 0).wait_send()
             relay(p, 1).wait_send()
@@ -598,6 +678,8 @@
                 *[notes] * 8,
                 *[pltpu.VMEM((pairs, rows, LANES), BF16)] * 4,
                 *[pltpu.VMEM((rows, channels), F32)] * 3,
+                pltpu.VMEM((HEADS, rows, rows), F32),
+                *[pltpu.VMEM((HEADS, rows, LANES), F32)] * 2,
                 pltpu.SemaphoreType.DMA((8,)),
                 *[pltpu.SemaphoreType.DMA((wide,))] * 8,
                 *[pltpu.SemaphoreType.DMA((2, pairs))] * 4,

time: 51.2 us -> 49.8 us (0.973)
  Pallas kernels: 50.1 us -> 48.4 us
    pallas_call x1, Pallas kernels: 50.1 us -> 48.4 us  [body(): pl.pallas_call(functools.partial(kernel, (wide, narrow, padded, per, shar...]
where the time goes in v3:
time: 49.8 us; the launch traced here: 49.2 us
  Pallas kernels  48.4 us (97%)
  local copies, waits for them, and re-layouts  0.8 us (2%)
    pallas_call x1, Pallas kernels, body(): pl.pallas_call(functools.partial(kernel, (wide, narrow, padded, per, shar...  48.4 us

profile of v3, /device:TPU:4, one launch (start us, length us, event | category | flops | bytes accessed | tf_op | source)
XLA Modules:
  0.0 49.2 jit_solution(3950366529210181791)
XLA Ops:
  0.0 48.4 %shard_map.82 = bf16[256,1024]{1,0:T(8,128)(2,1)S(1)} custom-call(bf16[256,256]{1,0:T(8,128)(2,1)} %fq_in.1, bf16[256,256]{1,0:T(8,128)(2,1)} %fk_in.1, bf16[256,1024]{1,0:T(8,128)(2,1)} %val_in.1, bf16[256,1024]{1,0:T(8,128)(2,1)} %wq_in.1, bf16[256,1024]{1,0:T(8,128)(2,1)} %wk_in.1, bf16[2,8,160,128]{3,2,1,0:T(8,128)(2,1)} %constant.6.clone.pick_in, ...), custom_call_target="tpu_custom_call" | custom-call | tf_op jit(solution)/shard_map/pallas_call | solution.py:668
  48.5 0.8 %copy.10 = bf16[256,1024]{1,0:T(8,128)(2,1)} copy(bf16[256,1024]{1,0:T(8,128)(2,1)S(1)} %shard_map.82) | data formatting | bytes 1048576

commit v4 on v3

--- a/solution.py
+++ b/solution.py
@@ -22,7 +22,7 @@
 BURST = 1
 RATE = 1
 LAG = 2
-FIRST = 2
+FIRST = 3
 DIRECT = 5
 KEEP = 0
 FINE = 65000.0
@@ -614,6 +614,13 @@
         def _():
             down(i).wait_send()
 
+    @pl.when(not_last & (mz == 0))
+    def _():
+        @pl.loop(0, pairs)
+        def _(p):
+            rim(p, 0).wait_send()
+            rim(p, 1).wait_send()
+
     turn = jnp.clip(DIRECT, soon, pairs)
 
     @pl.loop(soon, turn)
@@ -631,7 +638,7 @@
     def _(p):
         out[:, cols(p)] = (num[:, cols(p)] + finish(p)).astype(out.dtype)
 
-    @pl.when(not_last)
+    @pl.when(not_last & (mz > 0))
     def _():
         @pl.loop(0, pairs)
         def _(p):

time: 49.8 us -> 49.7 us (level)
  no operation moved by 1% of the time
where the time goes in v4:
time: 49.7 us; the launch traced here: 49.2 us
  Pallas kernels  48.4 us (97%)
  local copies, waits for them, and re-layouts  0.8 us (2%)
    pallas_call x1, Pallas kernels, body(): pl.pallas_call(functools.partial(kernel, (wide, narrow, padded, per, shar...  48.4 us

profile of v4, /device:TPU:4, one launch (start us, length us, event | category | flops | bytes accessed | tf_op | source)
XLA Modules:
  0.0 49.2 jit_solution(18186901521704331179)
XLA Ops:
  0.0 48.4 %shard_map.82 = bf16[256,1024]{1,0:T(8,128)(2,1)S(1)} custom-call(bf16[256,256]{1,0:T(8,128)(2,1)} %fq_in.1, bf16[256,256]{1,0:T(8,128)(2,1)} %fk_in.1, bf16[256,1024]{1,0:T(8,128)(2,1)} %val_in.1, bf16[256,1024]{1,0:T(8,128)(2,1)} %wq_in.1, bf16[256,1024]{1,0:T(8,128)(2,1)} %wk_in.1, bf16[2,8,160,128]{3,2,1,0:T(8,128)(2,1)} %constant.6.clone.pick_in, ...), custom_call_target="tpu_custom_call" | custom-call | tf_op jit(solution)/shard_map/pallas_call | solution.py:675
  48.4 0.8 %copy.10 = bf16[256,1024]{1,0:T(8,128)(2,1)} copy(bf16[256,1024]{1,0:T(8,128)(2,1)S(1)} %shard_map.82) | data formatting | bytes 1048576
